TPU v7x, 32 devices: a whole 2x2x4 slice. The times are simulated.
32 devices in a mesh: grp: 4 (over z), seq: 8 (over y, x, core).
Axes of the slice: x: 2, y: 2, z: 4, core: 2. Of those that a mesh axis runs over, the one named last changes fastest.
Arguments:
- latent: bfloat16 [4, 256, 32, 256], P('grp', 'seq'), may hold values from -6 to 6
- up_key: bfloat16 [4, 128, 256], replicated, may hold values from -0.5 to 0.5
- up_value: bfloat16 [4, 128, 256], replicated, may hold values from -0.5 to 0.5
- queries: bfloat16 [8, 64, 128], replicated, may hold values from -240 to 240, as said below
- lengths: int32 [8], replicated, may hold values from 1 to 1024
- block_dest: int32 [256], replicated, may hold values from 0 to 31, as said below
Outputs:
- decode_latent: bfloat16 [32, 4, 8, 32, 256], P(('grp', 'seq'))
- attended: float32 [8, 8192], replicated
Inputs may be any that keep to these rules, and one draw needn't show every extreme that they name: `block_dest`: each aligned run of 32 entries (the blocks of one seq index in the prefill layout) names every decode device exactly once. `queries`: the new token's query entries, real-valued.
All inputs are finite; a program needn't handle non-finite values.
Results may differ from a plain program's by a relative error of at most 0.001.
Values may be sent and summed in bfloat16 or wider, within the bound.
A program may use at most 64 MiB of HBM per device.

v0:
```python
import functools

import jax
import jax.numpy as jnp
from jax import lax
from jax.experimental import pallas as pl
from jax.experimental.pallas import tpu as pltpu
from jax.sharding import PartitionSpec as P

MESH = pl.DeviceIdType.MESH


def pieces(x):
    high = x.astype(jnp.bfloat16)
    rest = x - high.astype(jnp.float32)
    middle = rest.astype(jnp.bfloat16)
    low = (rest - middle.astype(jnp.float32)).astype(jnp.bfloat16)
    return jnp.concatenate([high, middle, low], axis=0)


def dot_pieces(x, y, dims):
    rows = x.shape[0]
    out = lax.dot_general(pieces(x), y, (dims, ((), ())), preferred_element_type=jnp.float32)
    return out[:rows] + (out[rows : 2 * rows] + out[2 * rows :])


def local_kernel(per_seq, per_group, per_kv, dest_ref, len_ref, lat_ref, q_ref, uk_ref, uv_ref, out_ref, part_ref):
    own_group = lax.axis_index("grp")
    own_shard = lax.axis_index("seq")
    slots, block_len, width = lat_ref.shape[1:]
    rank = width // 2
    head_dim = q_ref.shape[2]
    heads = per_group * per_kv

    @pl.loop(0, slots)
    def _(i):
        out_ref[dest_ref[own_shard * slots + i]] = lat_ref[0, i]

    sequence = own_shard // per_seq
    offset = (own_shard - sequence * per_seq) * (slots * block_len)
    left = len_ref[sequence] - offset
    tokens = slots * block_len
    query = q_ref[sequence, pl.ds(pl.multiple_of(own_group * heads, heads), heads), :]
    key_map = uk_ref[own_group]
    value_map = uv_ref[own_group]

    def cols(m, k):
        return m[:, k * head_dim : (k + 1) * head_dim]

    def rows(m, k):
        return m[k * per_kv : (k + 1) * per_kv]

    absorbed = jnp.concatenate(
        [
            rows(
                lax.dot_general(query, cols(key_map, k), (((1,), (1,)), ((), ())), preferred_element_type=jnp.float32),
                k,
            )
            for k in range(per_group)
        ],
        axis=0,
    )
    key_lat = lat_ref[0, :, :, :rank].reshape(tokens, rank)
    value_lat = lat_ref[0, :, :, rank:].reshape(tokens, rank)
    scores = dot_pieces(absorbed, key_lat, ((1,), (1,))) * (1.0 / float(head_dim) ** 0.5)
    live = lax.broadcasted_iota(jnp.int32, (heads, tokens), 1) < left
    scores = jnp.where(live, scores, -1e30)
    largest = jnp.max(scores, axis=1, keepdims=True)
    weights = jnp.where(live, jnp.exp(scores - largest), 0.0)
    total = jnp.sum(weights, axis=1, keepdims=True)
    some = jnp.where(total > 0.0, total, 1.0)
    mixed = dot_pieces(weights, value_lat, ((1,), (0,))) / some
    part_ref[0:heads, :] = jnp.concatenate(
        [rows(dot_pieces(mixed, cols(value_map, k), ((1,), (0,))), k) for k in range(per_group)], axis=0
    )
    if per_seq > 1:
        size = jnp.where(total > 0.0, largest + jnp.log(some), -1e30)
        part_ref[heads : 2 * heads, :] = jnp.broadcast_to(size, (heads, head_dim))


def comm_kernel(grps, seqs, out_ref, part_ref, recv_ref, all_ref, send_a, recv_a, send_b, recv_b, recv_z):
    n = grps * seqs
    group = lax.axis_index("grp")
    shard = lax.axis_index("seq")
    me = group * seqs + shard
    mine = shard * grps + group
    barrier = pltpu.get_barrier_semaphore()

    def place(k):
        to = lax.rem(me + k, n)
        return to, (to // seqs, lax.rem(to, seqs))

    def send(src, dst, there, send_sem, recv_sem):
        pltpu.make_async_remote_copy(
            src_ref=src, dst_ref=dst, send_sem=send_sem, recv_sem=recv_sem, device_id=there, device_id_type=MESH
        ).start()

    @pl.loop(1, n)
    def _(k):
        pl.semaphore_signal(barrier, inc=1, device_id=place(k)[1], device_id_type=MESH)

    pl.semaphore_wait(barrier, n - 1)

    @pl.loop(1, grps)
    def _(k):
        send(part_ref, all_ref.at[mine], (lax.rem(group + k, grps), shard), send_b, recv_z)

    def block(to_group, to_shard):
        send(out_ref.at[to_group * seqs + to_shard], recv_ref.at[me], (to_group, to_shard), send_a, recv_a)

    for j in range(grps - 1):
        step = 1 + (j + grps // 2 - 1) % (grps - 1)

        @pl.loop(0, seqs)
        def _(k):
            block(lax.rem(group + step, grps), lax.rem(shard + k, seqs))

    @pl.loop(1, seqs)
    def _(k):
        to_shard = lax.rem(shard + k, seqs)
        send(part_ref, all_ref.at[mine], (group, to_shard), send_b, recv_b)
        block(group, to_shard)

    recv_ref[me] = out_ref[me]
    all_ref[mine] = part_ref[...]

    def wait(ref, count, sem):
        some = ref.at[pl.ds(0, count)]
        pltpu.make_async_copy(some, some, sem).wait()

    wait(all_ref, grps - 1, recv_z)

    @pl.loop(1, grps)
    def _(j):
        held = all_ref.at[shard * grps + lax.rem(group + j, grps)]

        @pl.loop(1, seqs)
        def _(k):
            send(held, held, (group, lax.rem(shard + k, seqs)), send_b, recv_b)

    wait(all_ref, n - grps, recv_b)
    wait(recv_ref, n - 1, recv_a)
    wait(all_ref, n - 1, send_b)
    wait(recv_ref, n - 1, send_a)


def body(grps, seqs, latent, up_key, up_value, queries, lengths, block_dest):
    groups = up_key.shape[0]
    slots, block_len, width = latent.shape[1:]
    batch, q_heads, head_dim = queries.shape
    per_group = up_key.shape[2] // head_dim
    heads = q_heads // groups
    per_kv = heads // per_group
    n = grps * seqs
    blk_seq = block_dest.shape[0] // batch
    per_seq = blk_seq // slots
    assert per_seq * slots == blk_seq and n == slots and groups == grps
    part_rows = heads if per_seq == 1 else 2 * heads
    vmem = pl.BlockSpec(memory_space=pltpu.VMEM)
    smem = pl.BlockSpec(memory_space=pltpu.SMEM)
    outgoing, part = pl.pallas_call(
        functools.partial(local_kernel, per_seq, per_group, per_kv),
        out_shape=(
            jax.ShapeDtypeStruct((slots, block_len, width), latent.dtype),
            jax.ShapeDtypeStruct((part_rows, head_dim), jnp.float32),
        ),
        in_specs=[smem, smem, vmem, vmem, vmem, vmem],
        out_specs=(vmem, vmem),
        name="local_part",
    )(block_dest, lengths, latent, queries, up_key, up_value)
    received, everything = pl.pallas_call(
        functools.partial(comm_kernel, grps, seqs),
        out_shape=(
            jax.ShapeDtypeStruct((n, block_len, width), latent.dtype),
            jax.ShapeDtypeStruct((n, part_rows, head_dim), jnp.float32),
        ),
        in_specs=[vmem, vmem],
        out_specs=(vmem, vmem),
        scratch_shapes=[pltpu.SemaphoreType.DMA] * 5,
        compiler_params=pltpu.CompilerParams(collective_id=0, has_side_effects=True),
        name="exchange",
    )(outgoing, part)
    decode_latent = received.reshape(1, groups, seqs, block_len, width)
    parts = everything.reshape(batch, per_seq, groups, part_rows, head_dim)
    result = parts[:, 0, :, :heads]
    if per_seq > 1:
        share = jax.nn.softmax(parts[:, :, :, heads:], axis=1)
        result = jnp.sum(parts[:, :, :, :heads] * share, axis=1)
    attended = result.reshape(batch, q_heads * head_dim)
    return (decode_latent, attended)


def solution(mesh):
    return jax.shard_map(
        functools.partial(body, mesh.shape["grp"], mesh.shape["seq"]),
        mesh=mesh,
        in_specs=(P("grp", "seq", None, None), P(), P(), P(), P(), P()),
        out_specs=(P(("grp", "seq"), None, None, None, None), P()),
        check_vma=False,
    )
```

profile of v0, /device:TPU:11, one launch (start us, length us, event | category | flops | bytes accessed | tf_op | source)
XLA Modules:
  0.0 26.1 jit_solution(2077802195414509864)
XLA Ops:
  0.6 2.8 %local_part.1 = (bf16[32,32,256]{2,1,0:T(8,128)(2,1)}, f32[16,128]{1,0:T(8,128)}) custom-call(s32[256]{0:T(256)} %dest_ref.1, s32[8]{0:T(128)} %len_ref.1, bf16[1,32,32,256]{3,2,1,0:T(8,128)(2,1)} %lat_ref.1, bf16[8,64,128]{2,1,0:T(8,128)(2,1)} %q_ref.1, bf16[4,128,256]{2,1,0:T(8,128)(2,1)} %uk_ref.1, bf16[4,128,256]{2,1,0:T(8,128)(2,1)} %uv_ref.1), custom_call_target="tpu_custom_call" | custom-call | tf_op jit(solution)/shard_map/local_part/pallas_call | solution.py:161
  3.4 20.1 %exchange.1 = (bf16[32,32,256]{2,1,0:T(8,128)(2,1)}, f32[32,16,128]{2,1,0:T(8,128)}) custom-call(bf16[32,32,256]{2,1,0:T(8,128)(2,1)} %get-tuple-element.6.out_ref, f32[16,128]{1,0:T(8,128)} %get-tuple-element.7.part_ref), custom_call_target="tpu_custom_call" | custom-call | tf_op jit(solution)/shard_map/exchange/pallas_call | solution.py:171
  23.6 0.0 copy-start
  23.6 1.8 %reshape_squeeze_reshape.3 = f32[8,8192]{1,0:T(8,128)} reshape(f32[32,16,128]{2,1,0:T(8,128)} %get-tuple-element.9) | data formatting | bytes 524288 | tf_op jit(solution)/shard_map/reshape;squeeze;reshape | solution.py:189
  25.3 0.0 copy-done
  25.3 0.8 %copy.9 = bf16[1,4,8,32,256]{4,3,2,1,0:T(8,128)(2,1)} copy(bf16[1,4,8,32,256]{4,3,2,1,0:T(8,128)(2,1)S(1)} %bitcast.1) | data formatting | bytes 1048576
Async XLA Ops:
  23.6 1.8 %copy-start = (bf16[32,32,256]{2,1,0:T(8,128)(2,1)S(1)}, bf16[32,32,256]{2,1,0:T(8,128)(2,1)}, u32[]{:S(2)}) copy-start(bf16[32,32,256]{2,1,0:T(8,128)(2,1)} %get-tuple-element.8) | copy-start | bytes 1572868
where the time goes:
time: 26.3 us; the launch traced here: 26.1 us
  Pallas kernels  22.9 us (87%)
  local copies, waits for them, and re-layouts  2.56 us (10%)
  between operations  0.65 us (2%)
    pallas_call x1, Pallas kernels, body(): pl.pallas_call(functools.partial(comm_kernel, grps, seqs), out_shape=(jax...  20.1 us
    pallas_call x1, Pallas kernels, body(): pl.pallas_call(functools.partial(local_kernel, per_seq, per_group, per_kv...  2.79 us
    another operation x1, local copies, waits for them, and re-layouts, body(): attended = result.reshape(batch, q_heads * head_dim)  1.76 us
    unnamed x3, local copies, waits for them, and re-layouts  0.8 us

commit v1 on v0

v1 whole, which is shorter than its diff:
```python
import functools

import jax
import jax.numpy as jnp
from jax import lax
from jax.experimental import pallas as pl
from jax.experimental.pallas import tpu as pltpu
from jax.sharding import PartitionSpec as P

MESH = pl.DeviceIdType.MESH
CORES = 2


def pieces(x, count):
    parts = []
    for _ in range(count - 1):
        part = x.astype(jnp.bfloat16)
        parts.append(part)
        x = x - part.astype(jnp.float32)
    parts.append(x.astype(jnp.bfloat16))
    return jnp.concatenate(parts, axis=0)


def dot_pieces(x, y, dims, count):
    rows = x.shape[0]
    out = lax.dot_general(pieces(x, count), y, (dims, ((), ())), preferred_element_type=jnp.float32)
    total = out[(count - 1) * rows :]
    for k in range(count - 2, -1, -1):
        total = total + out[k * rows : (k + 1) * rows]
    return total


def attend(per_group, per_kv, left, scale, lat, q, uk, uv):
    slots, block_len, width = lat.shape
    rank = width // 2
    heads, head_dim = q.shape
    tokens = slots * block_len
    query = q[...]

    def cols(m, k):
        return m[:, k * head_dim : (k + 1) * head_dim]

    def rows(m, k):
        return m[k * per_kv : (k + 1) * per_kv]

    key_map = uk[...]
    value_map = uv[...]
    absorbed = jnp.concatenate(
        [
            rows(
                lax.dot_general(query, cols(key_map, k), (((1,), (1,)), ((), ())), preferred_element_type=jnp.float32),
                k,
            )
            for k in range(per_group)
        ],
        axis=0,
    )
    key_lat = lat[:, :, :rank].reshape(tokens, rank)
    value_lat = lat[:, :, rank:].reshape(tokens, rank)
    scores = dot_pieces(absorbed, key_lat, ((1,), (1,)), 3) * scale
    live = lax.broadcasted_iota(jnp.int32, (heads, tokens), 1) < left
    scores = jnp.where(live, scores, -1e30)
    largest = jnp.max(scores, axis=1, keepdims=True)
    weights = jnp.where(live, jnp.exp(scores - largest), 0.0)
    total = jnp.sum(weights, axis=1, keepdims=True)
    some = jnp.where(total > 0.0, total, 1.0)
    mixed = dot_pieces(weights, value_lat, ((1,), (0,)), 3) / some
    values = jnp.concatenate(
        [rows(dot_pieces(mixed, cols(value_map, k), ((1,), (0,)), 3), k) for k in range(per_group)], axis=0
    )
    return values, jnp.where(total > 0.0, largest + jnp.log(some), -1e30)


def kernel(
    grps,
    seqs,
    per_seq,
    per_group,
    per_kv,
    dest_hbm,
    len_hbm,
    lat_hbm,
    q_hbm,
    uk_hbm,
    uv_hbm,
    recv_ref,
    att_ref,
    dest_s,
    len_s,
    lat_v,
    q_v,
    uk_v,
    uv_v,
    out_v,
    part_v,
    all_v,
    in_sems,
    send_a,
    recv_a,
    send_z,
    recv_z,
    send_p,
    recv_p,
    send_c,
    recv_c,
    plane_sem,
):
    n = grps * seqs
    chips = seqs // CORES
    group = lax.axis_index("grp")
    shard = lax.axis_index("seq")
    me = group * seqs + shard
    spot = shard // CORES
    core = lax.rem(shard, CORES)
    slots, block_len, width = lat_v.shape
    heads, head_dim = q_v.shape
    barrier = pltpu.get_barrier_semaphore()

    def signal(sem, there):
        pl.semaphore_signal(sem, inc=1, device_id=there, device_id_type=MESH)

    def send(src, dst, there, send_sem, recv_sem):
        pltpu.make_async_remote_copy(
            src_ref=src, dst_ref=dst, send_sem=send_sem, recv_sem=recv_sem, device_id=there, device_id_type=MESH
        ).start()

    def wait(some, sem):
        pltpu.make_async_copy(some, some, sem).wait()

    for j in range(1, grps):
        there = lax.rem(group + j, grps)
        for c in range(CORES):
            signal(barrier, (there, spot * CORES + c))

    @pl.loop(1, seqs)
    def _(k):
        signal(barrier, (group, lax.rem(shard + k, seqs)))

    sequence = shard // per_seq
    loads = [
        (dest_hbm, dest_s),
        (lat_hbm.at[0], lat_v),
        (q_hbm.at[sequence, pl.ds(pl.multiple_of(group * heads, heads), heads)], q_v),
        (uk_hbm.at[group], uk_v),
        (uv_hbm.at[group], uv_v),
        (len_hbm, len_s),
    ]
    loads = [pltpu.make_async_copy(src, dst, in_sems.at[i]) for i, (src, dst) in enumerate(loads)]
    for load in loads:
        load.start()

    loads[0].wait()
    lanes = pl.cdiv(n, 128) * 128
    lane = lax.broadcasted_iota(jnp.int32, (1, lanes), 1)

    def place(i, held):
        return jnp.where(lane == dest_s[shard * slots + i], i, held)

    unroll = min(slots, 32)
    source = lax.fori_loop(0, slots, place, jnp.zeros((1, lanes), jnp.int32), unroll=unroll)
    loads[1].wait()

    def pick(d, _):
        out_v[d] = lat_v[jnp.sum(jnp.where(lane == d, source, 0))]
        return 0

    lax.fori_loop(0, n, pick, 0, unroll=unroll)
    recv_ref[me] = out_v[me]

    pl.semaphore_wait(barrier, (grps - 1) * CORES + seqs - 1)
    for k in range(1, chips):
        signal(plane_sem, (group, lax.rem(spot + k, chips) * CORES + core))

    def block(to_group, to_shard):
        send(out_v.at[to_group * seqs + to_shard], recv_ref.at[me], (to_group, to_shard), send_a, recv_a)

    order = [1 + (j + grps // 2 - 1) % (grps - 1) for j in range(grps - 1)]
    for step in order:
        for c in range(CORES):
            block(lax.rem(group + step, grps), spot * CORES + lax.rem(core + c, CORES))

    @pl.loop(1, seqs)
    def _(k):
        block(group, lax.rem(shard + k, seqs))

    for load in loads[2:]:
        load.wait()
    left = len_s[sequence] - (shard - sequence * per_seq) * (slots * block_len)
    values, size = attend(per_group, per_kv, left, 1.0 / float(head_dim) ** 0.5, lat_v, q_v, uk_v, uv_v)
    part_v[0:heads, :] = values
    if per_seq > 1:
        part_v[heads : 2 * heads, :] = jnp.broadcast_to(size, (heads, head_dim))
    all_v[spot, core, group] = part_v[...]

    for k in range(1, grps):
        send(part_v, all_v.at[spot, core, group], (lax.rem(group + k, grps), shard), send_z, recv_z)

    pl.semaphore_wait(plane_sem, chips - 1)
    for step in order:

        @pl.loop(CORES, seqs)
        def _(k):
            block(lax.rem(group + step, grps), lax.rem(spot * CORES + k, seqs))

    wait(all_v.at[0, 0, pl.ds(0, grps - 1)], recv_z)
    own = all_v.at[spot, core]
    for k in range(1, chips):
        send(own, own, (group, lax.rem(spot + k, chips) * CORES + core), send_p, recv_p)
    wait(all_v.at[pl.ds(0, chips - 1), 0], recv_p)
    half = all_v.at[:, core]
    for c in range(1, CORES):
        send(half, half, (group, spot * CORES + lax.rem(core + c, CORES)), send_c, recv_c)
    wait(all_v.at[:, pl.ds(0, CORES - 1)], recv_c)

    batch = att_ref.shape[0]
    for g in range(grps):
        if per_seq == 1:
            held = all_v[:, :, g].reshape(batch, heads, head_dim)
        else:
            part = all_v[:, :, g].reshape(batch, per_seq, 2 * heads, head_dim)
            sizes = part[:, :, heads:]
            share = jnp.exp(sizes - jnp.max(sizes, axis=1, keepdims=True))
            held = jnp.sum(part[:, :, :heads] * share, axis=1) / jnp.sum(share, axis=1)
        held = jnp.swapaxes(held, 0, 1)
        for h in range(heads):
            at = (g * heads + h) * head_dim
            att_ref[:, at : at + head_dim] = held[h]

    wait(recv_ref.at[pl.ds(0, n - 1)], recv_a)
    wait(recv_ref.at[pl.ds(0, n - 1)], send_a)
    wait(all_v.at[0, 0, pl.ds(0, grps - 1)], send_z)
    wait(all_v.at[pl.ds(0, chips - 1), 0], send_p)
    wait(all_v.at[:, pl.ds(0, CORES - 1)], send_c)


def write_kernel(recv_ref, att_ref, latent_out, attended_out, sems):
    copies = [
        pltpu.make_async_copy(recv_ref, latent_out, sems.at[0]),
        pltpu.make_async_copy(att_ref, attended_out, sems.at[1]),
    ]
    for copy in copies:
        copy.start()
    for copy in copies:
        copy.wait()


def body(grps, seqs, latent, up_key, up_value, queries, lengths, block_dest):
    groups, rank, maps = up_key.shape
    slots, block_len, width = latent.shape[1:]
    batch, q_heads, head_dim = queries.shape
    per_group = maps // head_dim
    heads = q_heads // groups
    per_kv = heads // per_group
    n = grps * seqs
    blk_seq = block_dest.shape[0] // batch
    per_seq = blk_seq // slots
    assert per_seq * slots == blk_seq and n == slots and groups == grps and seqs % CORES == 0
    part_rows = heads if per_seq == 1 else 2 * heads
    anywhere = pl.BlockSpec(memory_space=pl.ANY)
    vmem = pl.BlockSpec(memory_space=pltpu.VMEM)
    dma = pltpu.SemaphoreType.DMA
    received, attended = pl.pallas_call(
        functools.partial(kernel, grps, seqs, per_seq, per_group, per_kv),
        out_shape=(
            pltpu.VMEM((n, block_len, width), latent.dtype),
            pltpu.VMEM((batch, q_heads * head_dim), jnp.float32),
        ),
        in_specs=[anywhere] * 6,
        out_specs=(vmem, vmem),
        scratch_shapes=[
            pltpu.SMEM(block_dest.shape, jnp.int32),
            pltpu.SMEM(lengths.shape, jnp.int32),
            pltpu.VMEM((slots, block_len, width), latent.dtype),
            pltpu.VMEM((heads, head_dim), queries.dtype),
            pltpu.VMEM((rank, maps), up_key.dtype),
            pltpu.VMEM((rank, maps), up_value.dtype),
            pltpu.VMEM((n, block_len, width), latent.dtype),
            pltpu.VMEM((part_rows, head_dim), jnp.float32),
            pltpu.VMEM((seqs // CORES, CORES, grps, part_rows, head_dim), jnp.float32),
            dma((6,)),
        ]
        + [dma] * 8
        + [pltpu.SemaphoreType.REGULAR],
        compiler_params=pltpu.CompilerParams(collective_id=0, has_side_effects=True),
        name="exchange",
    )(block_dest, lengths, latent, queries, up_key, up_value)
    decode_latent, attended = pl.pallas_call(
        write_kernel,
        out_shape=(
            jax.ShapeDtypeStruct(received.shape, received.dtype),
            jax.ShapeDtypeStruct(attended.shape, attended.dtype),
        ),
        in_specs=[anywhere] * 2,
        out_specs=(anywhere, anywhere),
        scratch_shapes=[dma((2,))],
        name="write_out",
    )(pltpu.with_memory_space_constraint(received, pltpu.VMEM), pltpu.with_memory_space_constraint(attended, pltpu.VMEM))
    return (decode_latent.reshape(1, groups, seqs, block_len, width), attended)


def solution(mesh):
    return jax.shard_map(
        functools.partial(body, mesh.shape["grp"], mesh.shape["seq"]),
        mesh=mesh,
        in_specs=(P("grp", "seq", None, None), P(), P(), P(), P(), P()),
        out_specs=(P(("grp", "seq"), None, None, None, None), P()),
        check_vma=False,
    )
```

time: 26.3 us -> 20.5 us (0.78)
  the two profiles are of different devices: /device:TPU:11 before, /device:TPU:0 now
where the time goes in v1:
time: 20.5 us; the launch traced here: 20.4 us
  Pallas kernels  19.7 us (96%)
  between operations  0.64 us (3%)
    pallas_call x1, Pallas kernels, body(): pl.pallas_call(functools.partial(kernel, grps, seqs, per_seq, per_group,...  18.8 us
    pallas_call x1, Pallas kernels, body(): pl.pallas_call(write_kernel, out_shape=(jax.ShapeDtypeStruct(received.sha...  0.89 us

profile of v1, /device:TPU:0, one launch (start us, length us, event | category | flops | bytes accessed | tf_op | source)
XLA Modules:
  0.0 20.4 jit_solution(2281360245423937493)
XLA Ops:
  0.6 18.8 %exchange.1 = (bf16[32,32,256]{2,1,0:T(8,128)(2,1)S(1)}, f32[8,8192]{1,0:T(8,128)S(1)}) custom-call(s32[256]{0:T(256)} %dest_hbm.1, s32[8]{0:T(128)} %len_hbm.1, bf16[1,32,32,256]{3,2,1,0:T(8,128)(2,1)} %lat_hbm.1, bf16[8,64,128]{2,1,0:T(8,128)(2,1)} %q_hbm.1, bf16[4,128,256]{2,1,0:T(8,128)(2,1)} %uk_hbm.1, bf16[4,128,256]{2,1,0:T(8,128)(2,1)} %uv_hbm.1), custom_call_target="tpu_custom_call" | custom-call | tf_op jit(solution)/shard_map/exchange/pallas_call | solution.py:262
  19.5 0.9 %write_out.1 = (bf16[32,32,256]{2,1,0:T(8,128)(2,1)}, f32[8,8192]{1,0:T(8,128)}) custom-call(bf16[32,32,256]{2,1,0:T(8,128)(2,1)S(1)} %get-tuple-element.6.recv_ref, f32[8,8192]{1,0:T(8,128)S(1)} %get-tuple-element.7.att_ref), custom_call_target="tpu_custom_call" | custom-call | tf_op jit(solution)/shard_map/write_out/pallas_call | solution.py:287

commit v2 on v1

--- a/solution.py
+++ b/solution.py
@@ -1,4 +1,5 @@
 import functools
+import math
 
 import jax
 import jax.numpy as jnp
@@ -96,22 +97,34 @@
     all_v,
     in_sems,
     send_a,
-    recv_a,
+    recv_near,
+    recv_far,
     send_z,
     recv_z,
     send_p,
     recv_p,
     send_c,
     recv_c,
+    send_b,
+    recv_b,
     plane_sem,
+    line_sem,
+    all_sem,
+    go_sem,
 ):
     n = grps * seqs
     chips = seqs // CORES
+    half = grps // 2
     group = lax.axis_index("grp")
     shard = lax.axis_index("seq")
     me = group * seqs + shard
     spot = shard // CORES
     core = lax.rem(shard, CORES)
+    side = group // half
+    first_far = (1 - side) * half
+    leads = core == CORES - 1
+    last = (group == grps - 1) & (spot == chips - 1)
+    bits = [lax.rem(spot // 2**b, 2) for b in range(chips.bit_length() - 1)]
     slots, block_len, width = lat_v.shape
     heads, head_dim = q_v.shape
     barrier = pltpu.get_barrier_semaphore()
@@ -127,14 +140,14 @@
     def wait(some, sem):
         pltpu.make_async_copy(some, some, sem).wait()
 
-    for j in range(1, grps):
-        there = lax.rem(group + j, grps)
-        for c in range(CORES):
-            signal(barrier, (there, spot * CORES + c))
-
-    @pl.loop(1, seqs)
-    def _(k):
-        signal(barrier, (group, lax.rem(shard + k, seqs)))
+    def bits_in(v):
+        return sum(bit for b, bit in enumerate(bits) if v >> b & 1)
+
+    def count(of):
+        total = 1
+        for bit in bits:
+            total = total * of(bit)
+        return total
 
     sequence = shard // per_seq
     loads = [
@@ -146,10 +159,47 @@
         (len_hbm, len_s),
     ]
     loads = [pltpu.make_async_copy(src, dst, in_sems.at[i]) for i, (src, dst) in enumerate(loads)]
-    for load in loads:
+    for load in loads[:2]:
         load.start()
 
-    loads[0].wait()
+    with jax.named_scope("sig"):
+        for c in range(1, CORES):
+            signal(barrier, (group, spot * CORES + lax.rem(core + c, CORES)))
+        for v in range(chips):
+
+            @pl.when(bits_in(v) == 0)
+            def _():
+                @pl.loop(group + (1 if v == 0 else 0), grps)
+                def _(g):
+                    for c in range(CORES):
+                        signal(barrier, (g, (spot + v) * CORES + c))
+
+    for load in loads[2:]:
+        load.start()
+    with jax.named_scope("w_bar"):
+        pl.semaphore_wait(barrier, ((group + 1) * count(lambda bit: 1 + bit) - 1) * CORES + CORES - 1)
+
+    with jax.named_scope("sig2"):
+        for v in range(1, chips):
+
+            @pl.when(bits_in(v) == bin(v).count("1"))
+            def _():
+                signal(plane_sem, (group, (spot - v) * CORES + core))
+
+        @pl.when(group == half)
+        def _():
+            @pl.loop(0, half)
+            def _(g):
+                signal(line_sem, (g, shard))
+
+        @pl.when(last)
+        def _():
+            @pl.loop(0, grps * chips - 1)
+            def _(k):
+                signal(all_sem, (k // chips, lax.rem(k, chips) * CORES + core))
+
+    with jax.named_scope("w_dest"):
+        loads[0].wait()
     lanes = pl.cdiv(n, 128) * 128
     lane = lax.broadcasted_iota(jnp.int32, (1, lanes), 1)
 
@@ -158,79 +208,194 @@
 
     unroll = min(slots, 32)
     source = lax.fori_loop(0, slots, place, jnp.zeros((1, lanes), jnp.int32), unroll=unroll)
-    loads[1].wait()
+    with jax.named_scope("w_lat"):
+        loads[1].wait()
 
     def pick(d, _):
         out_v[d] = lat_v[jnp.sum(jnp.where(lane == d, source, 0))]
         return 0
 
-    lax.fori_loop(0, n, pick, 0, unroll=unroll)
-    recv_ref[me] = out_v[me]
-
-    pl.semaphore_wait(barrier, (grps - 1) * CORES + seqs - 1)
-    for k in range(1, chips):
-        signal(plane_sem, (group, lax.rem(spot + k, chips) * CORES + core))
-
-    def block(to_group, to_shard):
-        send(out_v.at[to_group * seqs + to_shard], recv_ref.at[me], (to_group, to_shard), send_a, recv_a)
-
-    order = [1 + (j + grps // 2 - 1) % (grps - 1) for j in range(grps - 1)]
-    for step in order:
-        for c in range(CORES):
-            block(lax.rem(group + step, grps), spot * CORES + lax.rem(core + c, CORES))
+    with jax.named_scope("pick"):
+        lax.fori_loop(0, n, pick, 0, unroll=unroll)
+        recv_ref[me] = out_v[me]
+
+    def block(to_group, to_shard, recv_sem):
+        send(out_v.at[to_group * seqs + to_shard], recv_ref.at[me], (to_group, to_shard), send_a, recv_sem)
+
+    def turn(table, k):
+        if table is None:
+            return lax.rem(spot + k, chips)
+        return sum(
+            row[k] * math.prod(bit if a >> b & 1 else 1 - bit for b, bit in enumerate(bits))
+            for a, row in enumerate(table)
+            if row[k]
+        )
+
+    upper_turns = ((0, 1, 2, 3), (0, 1, 3, 2), (0, 2, 1, 3), (1, 0, 2, 3)) if chips == 4 else None
+    lower_turns = ((0, 1, 2, 3), (1, 0, 3, 2), (2, 0, 1, 3), (3, 1, 0, 2)) if chips == 4 else None
+
+    def far_blocks(turns, j, first, end):
+        for k in range(first, end):
+            to_spot = turn(turns, k)
+            for c in range(CORES):
+                block(first_far + j, to_spot * CORES + lax.rem(core + c, CORES), recv_far)
+
+    def near_blocks(lowest, highest):
+        @pl.loop(lowest, highest)
+        def _(g):
+            @pl.loop(0, seqs)
+            def _(k):
+                block(g, lax.rem(shard + k, seqs), recv_near)
+
+    @pl.when(side == 1)
+    def _():
+        far_blocks(upper_turns, 0, 0, 1)
+
+    for load in loads[2:]:
+        load.wait()
+    with jax.named_scope("attend"):
+        left = len_s[sequence] - (shard - sequence * per_seq) * (slots * block_len)
+        values, size = attend(per_group, per_kv, left, 1.0 / float(head_dim) ** 0.5, lat_v, q_v, uk_v, uv_v)
+        part_v[0:heads, :] = values
+        if per_seq > 1:
+            part_v[heads : 2 * heads, :] = jnp.broadcast_to(size, (heads, head_dim))
+
+    @pl.when(core < CORES - 1)
+    def _():
+        send(part_v, all_v.at[spot, group, core], (group, spot * CORES + CORES - 1), send_c, recv_c)
+
+    @pl.when(leads)
+    def _():
+        all_v[spot, group, core] = part_v[...]
+
+    @pl.when(side == 0)
+    def _():
+        with jax.named_scope("w_line"):
+            pl.semaphore_wait(line_sem, 1)
+        far_blocks(lower_turns, 0, 0, 1)
+
+    with jax.named_scope("w_plane"):
+
+        @pl.when(spot < chips - 1)
+        def _():
+            pl.semaphore_wait(plane_sem, count(lambda bit: 2 - bit) - 1)
 
     @pl.loop(1, seqs)
     def _(k):
-        block(group, lax.rem(shard + k, seqs))
-
-    for load in loads[2:]:
-        load.wait()
-    left = len_s[sequence] - (shard - sequence * per_seq) * (slots * block_len)
-    values, size = attend(per_group, per_kv, left, 1.0 / float(head_dim) ** 0.5, lat_v, q_v, uk_v, uv_v)
-    part_v[0:heads, :] = values
-    if per_seq > 1:
-        part_v[heads : 2 * heads, :] = jnp.broadcast_to(size, (heads, head_dim))
-    all_v[spot, core, group] = part_v[...]
-
-    for k in range(1, grps):
-        send(part_v, all_v.at[spot, core, group], (lax.rem(group + k, grps), shard), send_z, recv_z)
-
-    pl.semaphore_wait(plane_sem, chips - 1)
-    for step in order:
-
-        @pl.loop(CORES, seqs)
-        def _(k):
-            block(lax.rem(group + step, grps), lax.rem(spot * CORES + k, seqs))
-
-    wait(all_v.at[0, 0, pl.ds(0, grps - 1)], recv_z)
-    own = all_v.at[spot, core]
-    for k in range(1, chips):
-        send(own, own, (group, lax.rem(spot + k, chips) * CORES + core), send_p, recv_p)
-    wait(all_v.at[pl.ds(0, chips - 1), 0], recv_p)
-    half = all_v.at[:, core]
-    for c in range(1, CORES):
-        send(half, half, (group, spot * CORES + lax.rem(core + c, CORES)), send_c, recv_c)
-    wait(all_v.at[:, pl.ds(0, CORES - 1)], recv_c)
+        block(group, lax.rem(shard + k, seqs), recv_near)
+
+    def along_line(g):
+        both = all_v.at[spot, group]
+        send(both, both, (g, shard), send_z, recv_z.at[group])
+
+    def over_plane(g):
+        both = all_v.at[spot, g]
+        for k in range(1, chips):
+            send(both, both, (group, lax.rem(spot + k, chips) * CORES + core), send_p, recv_p)
+
+    def release():
+        @pl.when(leads)
+        def _():
+            for c in range(CORES - 1):
+                signal(go_sem, (group, spot * CORES + c))
+
+        @pl.when(core < CORES - 1)
+        def _():
+            pl.semaphore_wait(go_sem, 1)
+
+    @pl.when(leads)
+    def _():
+        with jax.named_scope("w_part"):
+            wait(all_v.at[0, 0, pl.ds(0, CORES - 1)], recv_c)
+
+        @pl.loop(0, group)
+        def _(g):
+            along_line(g)
+
+    @pl.when(side == 1)
+    def _():
+        release()
+        for j in range(half):
+            far_blocks(upper_turns, j, 0 if j else 1, chips)
+
+    with jax.named_scope("w_all"):
+
+        @pl.when(jnp.logical_not(last))
+        def _():
+            pl.semaphore_wait(all_sem, 1)
+
+    @pl.when(leads)
+    def _():
+        @pl.loop(group + 1, grps)
+        def _(g):
+            along_line(g)
+
+        over_plane(group)
+
+    @pl.when(side == 0)
+    def _():
+        release()
+        for j in range(half):
+            far_blocks(lower_turns, j, 1, chips)
+        for j in range(1, half):
+            far_blocks(lower_turns, j, 0, 1)
+
+    near_blocks(side * half, group)
+    near_blocks(group + 1, (side + 1) * half)
+
+    @pl.when(leads)
+    def _():
+        for k in range(1, grps):
+            for g in (group - k, group + k):
+
+                @pl.when((g >= 0) & (g < grps))
+                def _():
+                    with jax.named_scope("w_z"):
+                        wait(all_v.at[0, 0], recv_z.at[g])
+                    over_plane(g)
+
+        with jax.named_scope("w_p"):
+            wait(all_v.at[pl.ds(0, chips - 1)], recv_p)
+        for c in range(CORES - 1):
+            send(all_v, all_v, (group, spot * CORES + c), send_b, recv_b)
+
+    @pl.when(core < CORES - 1)
+    def _():
+        with jax.named_scope("w_c"):
+            wait(all_v, recv_b)
 
     batch = att_ref.shape[0]
-    for g in range(grps):
-        if per_seq == 1:
-            held = all_v[:, :, g].reshape(batch, heads, head_dim)
-        else:
-            part = all_v[:, :, g].reshape(batch, per_seq, 2 * heads, head_dim)
-            sizes = part[:, :, heads:]
-            share = jnp.exp(sizes - jnp.max(sizes, axis=1, keepdims=True))
-            held = jnp.sum(part[:, :, :heads] * share, axis=1) / jnp.sum(share, axis=1)
-        held = jnp.swapaxes(held, 0, 1)
-        for h in range(heads):
-            at = (g * heads + h) * head_dim
-            att_ref[:, at : at + head_dim] = held[h]
-
-    wait(recv_ref.at[pl.ds(0, n - 1)], recv_a)
-    wait(recv_ref.at[pl.ds(0, n - 1)], send_a)
-    wait(all_v.at[0, 0, pl.ds(0, grps - 1)], send_z)
-    wait(all_v.at[pl.ds(0, chips - 1), 0], send_p)
-    wait(all_v.at[:, pl.ds(0, CORES - 1)], send_c)
+    with jax.named_scope("att"):
+        for g in range(grps):
+            if per_seq == 1:
+                held = all_v[:, g].reshape(batch, heads, head_dim)
+            else:
+                part = all_v[:, g].reshape(batch, per_seq, 2 * heads, head_dim)
+                sizes = part[:, :, heads:]
+                share = jnp.exp(sizes - jnp.max(sizes, axis=1, keepdims=True))
+                held = jnp.sum(part[:, :, :heads] * share, axis=1) / jnp.sum(share, axis=1)
+            held = jnp.swapaxes(held, 0, 1)
+            for h in range(heads):
+                at = (g * heads + h) * head_dim
+                att_ref[:, at : at + head_dim] = held[h]
+
+    with jax.named_scope("w_near"):
+        wait(recv_ref.at[pl.ds(0, n // 2 - 1)], recv_near)
+    with jax.named_scope("w_far"):
+        wait(recv_ref.at[pl.ds(0, n // 2)], recv_far)
+    with jax.named_scope("w_send"):
+        wait(recv_ref.at[pl.ds(0, n - 1)], send_a)
+
+    @pl.when(leads)
+    def _():
+        wait(all_v.at[0, pl.ds(0, grps - 1)], send_z)
+        wait(all_v.at[pl.ds(0, chips - 1)], send_p)
+        for c in range(CORES - 1):
+            wait(all_v, send_b)
+
+    @pl.when(core < CORES - 1)
+    def _():
+        wait(part_v, send_c)
 
 
 def write_kernel(recv_ref, att_ref, latent_out, attended_out, sems):
@@ -254,7 +419,8 @@
     n = grps * seqs
     blk_seq = block_dest.shape[0] // batch
     per_seq = blk_seq // slots
-    assert per_seq * slots == blk_seq and n == slots and groups == grps and seqs % CORES == 0
+    assert per_seq * slots == blk_seq and n == slots and groups == grps
+    assert grps % 2 == 0 and seqs % CORES == 0 and seqs // CORES & (seqs // CORES - 1) == 0
     part_rows = heads if per_seq == 1 else 2 * heads
     anywhere = pl.BlockSpec(memory_space=pl.ANY)
     vmem = pl.BlockSpec(memory_space=pltpu.VMEM)
@@ -276,11 +442,13 @@
             pltpu.VMEM((rank, maps), up_value.dtype),
             pltpu.VMEM((n, block_len, width), latent.dtype),
             pltpu.VMEM((part_rows, head_dim), jnp.float32),
-            pltpu.VMEM((seqs // CORES, CORES, grps, part_rows, head_dim), jnp.float32),
+            pltpu.VMEM((seqs // CORES, grps, CORES, part_rows, head_dim), jnp.float32),
             dma((6,)),
         ]
-        + [dma] * 8
-        + [pltpu.SemaphoreType.REGULAR],
+        + [dma] * 4
+        + [dma((grps,))]
+        + [dma] * 6
+        + [pltpu.SemaphoreType.REGULAR] * 4,
         compiler_params=pltpu.CompilerParams(collective_id=0, has_side_effects=True),
         name="exchange",
     )(block_dest, lengths, latent, queries, up_key, up_value)

time: 20.5 us -> 19.2 us (0.937)
  the two profiles are of different devices: /device:TPU:0 before, /device:TPU:13 now
where the time goes in v2:
time: 19.2 us; the launch traced here: 19 us
  Pallas kernels  18.3 us (95%)
  between operations  0.64 us (3%)
    pallas_call x1, Pallas kernels, body(): pl.pallas_call(functools.partial(kernel, grps, seqs, per_seq, per_group,...  17.5 us
    pallas_call x1, Pallas kernels, body(): pl.pallas_call(write_kernel, out_shape=(jax.ShapeDtypeStruct(received.sha...  0.89 us

profile of v2, /device:TPU:13, one launch (start us, length us, event | category | flops | bytes accessed | tf_op | source)
XLA Modules:
  0.0 19.0 jit_solution(10108927571823649523)
XLA Ops:
  0.6 17.5 %exchange.1 = (bf16[32,32,256]{2,1,0:T(8,128)(2,1)S(1)}, f32[8,8192]{1,0:T(8,128)S(1)}) custom-call(s32[256]{0:T(256)} %dest_hbm.1, s32[8]{0:T(128)} %len_hbm.1, bf16[1,32,32,256]{3,2,1,0:T(8,128)(2,1)} %lat_hbm.1, bf16[8,64,128]{2,1,0:T(8,128)(2,1)} %q_hbm.1, bf16[4,128,256]{2,1,0:T(8,128)(2,1)} %uk_hbm.1, bf16[4,128,256]{2,1,0:T(8,128)(2,1)} %uv_hbm.1), custom_call_target="tpu_custom_call" | custom-call | tf_op jit(solution)/shard_map/exchange/pallas_call | solution.py:428
  18.1 0.9 %write_out.1 = (bf16[32,32,256]{2,1,0:T(8,128)(2,1)}, f32[8,8192]{1,0:T(8,128)}) custom-call(bf16[32,32,256]{2,1,0:T(8,128)(2,1)S(1)} %get-tuple-element.6.recv_ref, f32[8,8192]{1,0:T(8,128)S(1)} %get-tuple-element.7.att_ref), custom_call_target="tpu_custom_call" | custom-call | tf_op jit(solution)/shard_map/write_out/pallas_call | solution.py:455

commit v3 on v2

--- a/solution.py
+++ b/solution.py
@@ -88,6 +88,7 @@
     att_ref,
     dest_s,
     len_s,
+    from_s,
     lat_v,
     q_v,
     uk_v,
@@ -111,6 +112,8 @@
     line_sem,
     all_sem,
     go_sem,
+    top_sem,
+    mid_sem,
 ):
     n = grps * seqs
     chips = seqs // CORES
@@ -192,6 +195,18 @@
             def _(g):
                 signal(line_sem, (g, shard))
 
+        @pl.when(group == grps - 1)
+        def _():
+            @pl.loop(0, grps - 1)
+            def _(g):
+                signal(top_sem, (g, shard))
+
+        @pl.when((group == half) & (spot == chips - 1))
+        def _():
+            @pl.loop(0, half * chips)
+            def _(k):
+                signal(mid_sem, (k // chips, lax.rem(k, chips) * CORES + core))
+
         @pl.when(last)
         def _():
             @pl.loop(0, grps * chips - 1)
@@ -208,11 +223,17 @@
 
     unroll = min(slots, 32)
     source = lax.fori_loop(0, slots, place, jnp.zeros((1, lanes), jnp.int32), unroll=unroll)
+
+    def find(d, _):
+        from_s[d] = jnp.sum(jnp.where(lane == d, source, 0))
+        return 0
+
+    lax.fori_loop(0, n, find, 0, unroll=unroll)
     with jax.named_scope("w_lat"):
         loads[1].wait()
 
     def pick(d, _):
-        out_v[d] = lat_v[jnp.sum(jnp.where(lane == d, source, 0))]
+        out_v[d] = lat_v[from_s[d]]
         return 0
 
     with jax.named_scope("pick"):
@@ -231,8 +252,12 @@
             if row[k]
         )
 
-    upper_turns = ((0, 1, 2, 3), (0, 1, 3, 2), (0, 2, 1, 3), (1, 0, 2, 3)) if chips == 4 else None
-    lower_turns = ((0, 1, 2, 3), (1, 0, 3, 2), (2, 0, 1, 3), (3, 1, 0, 2)) if chips == 4 else None
+    if chips == 4:
+        upper_turns = ((0, 1, 2, 3), (0, 1, 3, 2), (0, 2, 1, 3), (1, 0, 2, 3))
+        lower_turns = ((0, 1, 2, 3), (1, 0, 3, 2), (2, 3, 0, 1), (3, 0, 1, 2))
+    else:
+        upper_turns = lower_turns = None
+    ahead = (spot > 0) & (core < CORES - 1) & (chips == 4)
 
     def far_blocks(turns, j, first, end):
         for k in range(first, end):
@@ -250,6 +275,10 @@
     @pl.when(side == 1)
     def _():
         far_blocks(upper_turns, 0, 0, 1)
+
+        @pl.when(ahead)
+        def _():
+            far_blocks(upper_turns, 0, 1, 2)
 
     for load in loads[2:]:
         load.wait()
@@ -312,33 +341,61 @@
         def _(g):
             along_line(g)
 
+    def parts_up():
+        with jax.named_scope("w_top"):
+
+            @pl.when(group < grps - 1)
+            def _():
+                pl.semaphore_wait(top_sem, 1)
+
+        @pl.when(leads)
+        def _():
+            @pl.loop(group + 1, grps)
+            def _(g):
+                along_line(g)
+
     @pl.when(side == 1)
     def _():
         release()
-        for j in range(half):
-            far_blocks(upper_turns, j, 0 if j else 1, chips)
-
-    with jax.named_scope("w_all"):
-
-        @pl.when(jnp.logical_not(last))
-        def _():
-            pl.semaphore_wait(all_sem, 1)
-
-    @pl.when(leads)
-    def _():
-        @pl.loop(group + 1, grps)
-        def _(g):
-            along_line(g)
-
-        over_plane(group)
-
-    @pl.when(side == 0)
-    def _():
-        release()
-        for j in range(half):
+
+        @pl.when(jnp.logical_not(ahead))
+        def _():
+            far_blocks(upper_turns, 0, 1, 2)
+
+        far_blocks(upper_turns, 0, 2, chips)
+        for j in range(1, half):
             far_blocks(lower_turns, j, 1, chips)
         for j in range(1, half):
             far_blocks(lower_turns, j, 0, 1)
+
+    @pl.when(side == 0)
+    def _():
+        parts_up()
+        release()
+        with jax.named_scope("w_mid"):
+            pl.semaphore_wait(mid_sem, 1)
+        far_blocks(lower_turns, 0, 1, chips)
+
+    with jax.named_scope("w_all"):
+
+        @pl.when(jnp.logical_not(last))
+        def _():
+            pl.semaphore_wait(all_sem, 1)
+
+    @pl.when(side == 0)
+    def _():
+        for j in range(1, half):
+            far_blocks(lower_turns, j, 1, chips)
+        for j in range(1, half):
+            far_blocks(lower_turns, j, 0, 1)
+
+    @pl.when(side == 1)
+    def _():
+        parts_up()
+
+    @pl.when(leads)
+    def _():
+        over_plane(group)
 
     near_blocks(side * half, group)
     near_blocks(group + 1, (side + 1) * half)
@@ -379,23 +436,24 @@
                 at = (g * heads + h) * head_dim
                 att_ref[:, at : at + head_dim] = held[h]
 
+    with jax.named_scope("w_send"):
+        wait(recv_ref.at[pl.ds(0, n - 1)], send_a)
+
+    @pl.when(leads)
+    def _():
+        wait(all_v.at[0, pl.ds(0, grps - 1)], send_z)
+        wait(all_v.at[pl.ds(0, chips - 1)], send_p)
+        for c in range(CORES - 1):
+            wait(all_v, send_b)
+
+    @pl.when(core < CORES - 1)
+    def _():
+        wait(part_v, send_c)
+
     with jax.named_scope("w_near"):
         wait(recv_ref.at[pl.ds(0, n // 2 - 1)], recv_near)
     with jax.named_scope("w_far"):
         wait(recv_ref.at[pl.ds(0, n // 2)], recv_far)
-    with jax.named_scope("w_send"):
-        wait(recv_ref.at[pl.ds(0, n - 1)], send_a)
-
-    @pl.when(leads)
-    def _():
-        wait(all_v.at[0, pl.ds(0, grps - 1)], send_z)
-        wait(all_v.at[pl.ds(0, chips - 1)], send_p)
-        for c in range(CORES - 1):
-            wait(all_v, send_b)
-
-    @pl.when(core < CORES - 1)
-    def _():
-        wait(part_v, send_c)
 
 
 def write_kernel(recv_ref, att_ref, latent_out, attended_out, sems):
@@ -436,6 +494,7 @@
         scratch_shapes=[
             pltpu.SMEM(block_dest.shape, jnp.int32),
             pltpu.SMEM(lengths.shape, jnp.int32),
+            pltpu.SMEM((n,), jnp.int32),
             pltpu.VMEM((slots, block_len, width), latent.dtype),
             pltpu.VMEM((heads, head_dim), queries.dtype),
             pltpu.VMEM((rank, maps), up_key.dtype),
@@ -448,7 +507,7 @@
         + [dma] * 4
         + [dma((grps,))]
         + [dma] * 6
-        + [pltpu.SemaphoreType.REGULAR] * 4,
+        + [pltpu.SemaphoreType.REGULAR] * 6,
         compiler_params=pltpu.CompilerParams(collective_id=0, has_side_effects=True),
         name="exchange",
     )(block_dest, lengths, latent, queries, up_key, up_value)

time: 19.2 us -> 18.5 us (0.964)
  Pallas kernels: 18.3 us -> 17.6 us
    pallas_call x1, Pallas kernels: 17.5 us -> 16.7 us  [body(): pl.pallas_call(functools.partial(kernel, grps, seqs, per_seq, per_group,...]
where the time goes in v3:
time: 18.5 us; the launch traced here: 18.3 us
  Pallas kernels  17.6 us (95%)
  between operations  0.64 us (3%)
    pallas_call x1, Pallas kernels, body(): pl.pallas_call(functools.partial(kernel, grps, seqs, per_seq, per_group,...  16.7 us
    pallas_call x1, Pallas kernels, body(): pl.pallas_call(write_kernel, out_shape=(jax.ShapeDtypeStruct(received.sha...  0.89 us

profile of v3, /device:TPU:13, one launch (start us, length us, event | category | flops | bytes accessed | tf_op | source)
XLA Modules:
  0.0 18.3 jit_solution(16703263846883119257)
XLA Ops:
  0.6 16.7 %exchange.1 = (bf16[32,32,256]{2,1,0:T(8,128)(2,1)S(1)}, f32[8,8192]{1,0:T(8,128)S(1)}) custom-call(s32[256]{0:T(256)} %dest_hbm.1, s32[8]{0:T(128)} %len_hbm.1, bf16[1,32,32,256]{3,2,1,0:T(8,128)(2,1)} %lat_hbm.1, bf16[8,64,128]{2,1,0:T(8,128)(2,1)} %q_hbm.1, bf16[4,128,256]{2,1,0:T(8,128)(2,1)} %uk_hbm.1, bf16[4,128,256]{2,1,0:T(8,128)(2,1)} %uv_hbm.1), custom_call_target="tpu_custom_call" | custom-call | tf_op jit(solution)/shard_map/exchange/pallas_call | solution.py:486
  17.4 0.9 %write_out.1 = (bf16[32,32,256]{2,1,0:T(8,128)(2,1)}, f32[8,8192]{1,0:T(8,128)}) custom-call(bf16[32,32,256]{2,1,0:T(8,128)(2,1)S(1)} %get-tuple-element.6.recv_ref, f32[8,8192]{1,0:T(8,128)S(1)} %get-tuple-element.7.att_ref), custom_call_target="tpu_custom_call" | custom-call | tf_op jit(solution)/shard_map/write_out/pallas_call | solution.py:514

commit v4 on v3

--- a/solution.py
+++ b/solution.py
@@ -257,6 +257,7 @@
         lower_turns = ((0, 1, 2, 3), (1, 0, 3, 2), (2, 3, 0, 1), (3, 0, 1, 2))
     else:
         upper_turns = lower_turns = None
+    ahead_own = (spot == 0) & (core < CORES - 1)
     ahead = (spot > 0) & (core < CORES - 1) & (chips == 4)
 
     def far_blocks(turns, j, first, end):
@@ -279,6 +280,11 @@
         @pl.when(ahead)
         def _():
             far_blocks(upper_turns, 0, 1, 2)
+
+        @pl.when(ahead_own)
+        def _():
+            for j in range(1, half):
+                far_blocks(lower_turns, j, 0, 1)
 
     for load in loads[2:]:
         load.wait()
@@ -332,6 +338,10 @@
         def _():
             pl.semaphore_wait(go_sem, 1)
 
+    @pl.when(core < CORES - 1)
+    def _():
+        near_blocks(side * half, group)
+
     @pl.when(leads)
     def _():
         with jax.named_scope("w_part"):
@@ -341,6 +351,8 @@
         def _(g):
             along_line(g)
 
+        near_blocks(side * half, group)
+
     def parts_up():
         with jax.named_scope("w_top"):
 
@@ -363,42 +375,45 @@
             far_blocks(upper_turns, 0, 1, 2)
 
         far_blocks(upper_turns, 0, 2, chips)
+        for j in range(1, half):
+            far_blocks(lower_turns, j, 1, chips)
+
+        @pl.when(jnp.logical_not(ahead_own))
+        def _():
+            for j in range(1, half):
+                far_blocks(lower_turns, j, 0, 1)
+
+    @pl.when(side == 0)
+    def _():
+        parts_up()
+        release()
+        with jax.named_scope("w_mid"):
+            pl.semaphore_wait(mid_sem, 1)
+        near_blocks(group + 1, half)
+        far_blocks(lower_turns, 0, 1, chips)
+
+    with jax.named_scope("w_all"):
+
+        @pl.when(jnp.logical_not(last))
+        def _():
+            pl.semaphore_wait(all_sem, 1)
+
+    @pl.when(side == 0)
+    def _():
         for j in range(1, half):
             far_blocks(lower_turns, j, 1, chips)
         for j in range(1, half):
             far_blocks(lower_turns, j, 0, 1)
 
-    @pl.when(side == 0)
+    @pl.when(side == 1)
     def _():
         parts_up()
-        release()
-        with jax.named_scope("w_mid"):
-            pl.semaphore_wait(mid_sem, 1)
-        far_blocks(lower_turns, 0, 1, chips)
-
-    with jax.named_scope("w_all"):
-
-        @pl.when(jnp.logical_not(last))
-        def _():
-            pl.semaphore_wait(all_sem, 1)
-
-    @pl.when(side == 0)
-    def _():
-        for j in range(1, half):
-            far_blocks(lower_turns, j, 1, chips)
-        for j in range(1, half):
-            far_blocks(lower_turns, j, 0, 1)
-
-    @pl.when(side == 1)
-    def _():
-        parts_up()
+        near_blocks(group + 1, grps)
 
     @pl.when(leads)
     def _():
         over_plane(group)
 
-    near_blocks(side * half, group)
-    near_blocks(group + 1, (side + 1) * half)
 
     @pl.when(leads)
     def _():

time: 18.5 us -> 18.4 us (level)
  no operation moved by 1% of the time
where the time goes in v4:
time: 18.4 us; the launch traced here: 18.3 us
  Pallas kernels  17.6 us (96%)
  between operations  0.64 us (3%)
    pallas_call x1, Pallas kernels, body(): pl.pallas_call(functools.partial(kernel, grps, seqs, per_seq, per_group,...  16.7 us
    pallas_call x1, Pallas kernels, body(): pl.pallas_call(write_kernel, out_shape=(jax.ShapeDtypeStruct(received.sha...  0.89 us

profile of v4, /device:TPU:13, one launch (start us, length us, event | category | flops | bytes accessed | tf_op | source)
XLA Modules:
  0.0 18.3 jit_solution(8552135224303124491)
XLA Ops:
  0.6 16.7 %exchange.1 = (bf16[32,32,256]{2,1,0:T(8,128)(2,1)S(1)}, f32[8,8192]{1,0:T(8,128)S(1)}) custom-call(s32[256]{0:T(256)} %dest_hbm.1, s32[8]{0:T(128)} %len_hbm.1, bf16[1,32,32,256]{3,2,1,0:T(8,128)(2,1)} %lat_hbm.1, bf16[8,64,128]{2,1,0:T(8,128)(2,1)} %q_hbm.1, bf16[4,128,256]{2,1,0:T(8,128)(2,1)} %uk_hbm.1, bf16[4,128,256]{2,1,0:T(8,128)(2,1)} %uv_hbm.1), custom_call_target="tpu_custom_call" | custom-call | tf_op jit(solution)/shard_map/exchange/pallas_call | solution.py:501
  17.4 0.9 %write_out.1 = (bf16[32,32,256]{2,1,0:T(8,128)(2,1)}, f32[8,8192]{1,0:T(8,128)}) custom-call(bf16[32,32,256]{2,1,0:T(8,128)(2,1)S(1)} %get-tuple-element.6.recv_ref, f32[8,8192]{1,0:T(8,128)S(1)} %get-tuple-element.7.att_ref), custom_call_target="tpu_custom_call" | custom-call | tf_op jit(solution)/shard_map/write_out/pallas_call | solution.py:529

commit v5 on v4

--- a/solution.py
+++ b/solution.py
@@ -108,6 +108,8 @@
     recv_c,
     send_b,
     recv_b,
+    send_x,
+    send_d,
     plane_sem,
     line_sem,
     all_sem,
@@ -126,6 +128,8 @@
     side = group // half
     first_far = (1 - side) * half
     leads = core == CORES - 1
+    outer = (group == 0) | (group == grps - 1)
+    inner = (group > 0) & (group < grps - 1)
     last = (group == grps - 1) & (spot == chips - 1)
     bits = [lax.rem(spot // 2**b, 2) for b in range(chips.bit_length() - 1)]
     slots, block_len, width = lat_v.shape
@@ -295,6 +299,10 @@
         if per_seq > 1:
             part_v[heads : 2 * heads, :] = jnp.broadcast_to(size, (heads, head_dim))
 
+    @pl.loop(side * half, group)
+    def _(g):
+        send(part_v, all_v.at[spot, group, core], (g, spot * CORES + CORES - 1), send_d, recv_z.at[group])
+
     @pl.when(core < CORES - 1)
     def _():
         send(part_v, all_v.at[spot, group, core], (group, spot * CORES + CORES - 1), send_c, recv_c)
@@ -333,6 +341,7 @@
         def _():
             for c in range(CORES - 1):
                 signal(go_sem, (group, spot * CORES + c))
+            over_plane(group)
 
         @pl.when(core < CORES - 1)
         def _():
@@ -347,9 +356,9 @@
         with jax.named_scope("w_part"):
             wait(all_v.at[0, 0, pl.ds(0, CORES - 1)], recv_c)
 
-        @pl.loop(0, group)
-        def _(g):
-            along_line(g)
+        @pl.when(side == 1)
+        def _():
+            along_line(0)
 
         near_blocks(side * half, group)
 
@@ -362,13 +371,31 @@
 
         @pl.when(leads)
         def _():
-            @pl.loop(group + 1, grps)
+            @pl.loop(group + 1, (side + 1) * half)
             def _(g):
                 along_line(g)
 
+            @pl.when(side == 0)
+            def _():
+                along_line(grps - 1)
+
+    def pass_on():
+        @pl.when(leads & outer)
+        def _():
+            for k in range(half):
+                g = first_far + k
+                with jax.named_scope("w_x"):
+                    wait(all_v.at[0, 0], recv_z.at[g])
+                crossed = all_v.at[spot, g]
+                for i in range(1, half):
+                    to_group = side * half + lax.rem(group - side * half + i, half)
+                    send(crossed, crossed, (to_group, shard), send_x, recv_z.at[g])
+                over_plane(g)
+
     @pl.when(side == 1)
     def _():
         release()
+        pass_on()
 
         @pl.when(jnp.logical_not(ahead))
         def _():
@@ -390,6 +417,7 @@
         with jax.named_scope("w_mid"):
             pl.semaphore_wait(mid_sem, 1)
         near_blocks(group + 1, half)
+        pass_on()
         far_blocks(lower_turns, 0, 1, chips)
 
     with jax.named_scope("w_all"):
@@ -410,17 +438,13 @@
         parts_up()
         near_blocks(group + 1, grps)
 
-    @pl.when(leads)
-    def _():
-        over_plane(group)
-
 
     @pl.when(leads)
     def _():
         for k in range(1, grps):
             for g in (group - k, group + k):
 
-                @pl.when((g >= 0) & (g < grps))
+                @pl.when((g >= 0) & (g < grps) & (inner | ((g >= side * half) & (g < (side + 1) * half))))
                 def _():
                     with jax.named_scope("w_z"):
                         wait(all_v.at[0, 0], recv_z.at[g])
@@ -456,7 +480,16 @@
 
     @pl.when(leads)
     def _():
-        wait(all_v.at[0, pl.ds(0, grps - 1)], send_z)
+        @pl.loop(0, half - (group - side * half))
+        def _(_):
+            wait(all_v.at[0, 0], send_z)
+
+
+        @pl.when(outer)
+        def _():
+            for _ in range(half - 1):
+                wait(all_v.at[0, pl.ds(0, half)], send_x)
+
         wait(all_v.at[pl.ds(0, chips - 1)], send_p)
         for c in range(CORES - 1):
             wait(all_v, send_b)
@@ -464,6 +497,10 @@
     @pl.when(core < CORES - 1)
     def _():
         wait(part_v, send_c)
+
+    @pl.loop(side * half, group)
+    def _(_):
+        wait(part_v, send_d)
 
     with jax.named_scope("w_near"):
         wait(recv_ref.at[pl.ds(0, n // 2 - 1)], recv_near)
@@ -521,7 +558,7 @@
         ]
         + [dma] * 4
         + [dma((grps,))]
-        + [dma] * 6
+        + [dma] * 8
         + [pltpu.SemaphoreType.REGULAR] * 6,
         compiler_params=pltpu.CompilerParams(collective_id=0, has_side_effects=True),
         name="exchange",

time: 18.4 us -> 18 us (0.978)
  Pallas kernels: 17.6 us -> 17.2 us
    pallas_call x1, Pallas kernels: 16.7 us -> 16.3 us  [body(): pl.pallas_call(functools.partial(kernel, grps, seqs, per_seq, per_group,...]
where the time goes in v5:
time: 18 us; the launch traced here: 17.8 us
  Pallas kernels  17.2 us (96%)
  between operations  0.64 us (4%)
    pallas_call x1, Pallas kernels, body(): pl.pallas_call(functools.partial(kernel, grps, seqs, per_seq, per_group,...  16.3 us
    pallas_call x1, Pallas kernels, body(): pl.pallas_call(write_kernel, out_shape=(jax.ShapeDtypeStruct(received.sha...  0.89 us

profile of v5, /device:TPU:13, one launch (start us, length us, event | category | flops | bytes accessed | tf_op | source)
XLA Modules:
  0.0 17.8 jit_solution(3412920687476000168)
XLA Ops:
  0.6 16.3 %exchange.1 = (bf16[32,32,256]{2,1,0:T(8,128)(2,1)S(1)}, f32[8,8192]{1,0:T(8,128)S(1)}) custom-call(s32[256]{0:T(256)} %dest_hbm.1, s32[8]{0:T(128)} %len_hbm.1, bf16[1,32,32,256]{3,2,1,0:T(8,128)(2,1)} %lat_hbm.1, bf16[8,64,128]{2,1,0:T(8,128)(2,1)} %q_hbm.1, bf16[4,128,256]{2,1,0:T(8,128)(2,1)} %uk_hbm.1, bf16[4,128,256]{2,1,0:T(8,128)(2,1)} %uv_hbm.1), custom_call_target="tpu_custom_call" | custom-call | tf_op jit(solution)/shard_map/exchange/pallas_call | solution.py:538
  16.9 0.9 %write_out.1 = (bf16[32,32,256]{2,1,0:T(8,128)(2,1)}, f32[8,8192]{1,0:T(8,128)}) custom-call(bf16[32,32,256]{2,1,0:T(8,128)(2,1)S(1)} %get-tuple-element.6.recv_ref, f32[8,8192]{1,0:T(8,128)S(1)} %get-tuple-element.7.att_ref), custom_call_target="tpu_custom_call" | custom-call | tf_op jit(solution)/shard_map/write_out/pallas_call | solution.py:566

commit v6 on v5

--- a/solution.py
+++ b/solution.py
@@ -94,6 +94,7 @@
     uk_v,
     uv_v,
     out_v,
+    relay_v,
     part_v,
     all_v,
     in_sems,
@@ -110,6 +111,8 @@
     recv_b,
     send_x,
     send_d,
+    send_r,
+    recv_r,
     plane_sem,
     line_sem,
     all_sem,
@@ -258,7 +261,7 @@
 
     if chips == 4:
         upper_turns = ((0, 1, 2, 3), (0, 1, 3, 2), (0, 2, 1, 3), (1, 0, 2, 3))
-        lower_turns = ((0, 1, 2, 3), (1, 0, 3, 2), (2, 3, 0, 1), (3, 0, 1, 2))
+        lower_turns = ((0, 3, 1, 2), (1, 2, 0, 3), (2, 1, 0, 3), (3, 0, 1, 2))
     else:
         upper_turns = lower_turns = None
     ahead_own = (spot == 0) & (core < CORES - 1)
@@ -269,6 +272,31 @@
             to_spot = turn(turns, k)
             for c in range(CORES):
                 block(first_far + j, to_spot * CORES + lax.rem(core + c, CORES), recv_far)
+
+    detour = lower_turns is not None and half > 1
+    turns_off = (group == half - 1 + side) & (spot == chips - 1) & (core == side)
+    relays = (group == half - 1 + side) & (spot == 0) & (core == side)
+    off_spot = lower_turns[-1][-1] if detour else 0
+    off_group = first_far + half - 1
+
+    def later_blocks():
+        for j in range(1, half):
+            far_blocks(lower_turns, j, 1, chips - 1)
+            if not detour or j < half - 1:
+                far_blocks(lower_turns, j, chips - 1, chips)
+        if detour:
+
+            @pl.when(jnp.logical_not(turns_off))
+            def _():
+                far_blocks(lower_turns, half - 1, chips - 1, chips)
+
+            @pl.when(relays)
+            def _():
+                wait(relay_v, recv_r)
+                source_row = group * seqs + (chips - 1) * CORES + core
+                for c in range(CORES):
+                    there = (off_group, off_spot * CORES + c)
+                    send(relay_v.at[c], recv_ref.at[source_row], there, send_r, recv_far)
 
     def near_blocks(lowest, highest):
         @pl.loop(lowest, highest)
@@ -322,6 +350,14 @@
         @pl.when(spot < chips - 1)
         def _():
             pl.semaphore_wait(plane_sem, count(lambda bit: 2 - bit) - 1)
+
+    if detour:
+
+        @pl.when(turns_off)
+        def _():
+            for c in range(CORES):
+                held = out_v.at[off_group * seqs + off_spot * CORES + c]
+                send(held, relay_v.at[c], (group, core), send_a, recv_r)
 
     @pl.loop(1, seqs)
     def _(k):
@@ -402,8 +438,7 @@
             far_blocks(upper_turns, 0, 1, 2)
 
         far_blocks(upper_turns, 0, 2, chips)
-        for j in range(1, half):
-            far_blocks(lower_turns, j, 1, chips)
+        later_blocks()
 
         @pl.when(jnp.logical_not(ahead_own))
         def _():
@@ -428,8 +463,7 @@
 
     @pl.when(side == 0)
     def _():
-        for j in range(1, half):
-            far_blocks(lower_turns, j, 1, chips)
+        later_blocks()
         for j in range(1, half):
             far_blocks(lower_turns, j, 0, 1)
 
@@ -493,6 +527,12 @@
         wait(all_v.at[pl.ds(0, chips - 1)], send_p)
         for c in range(CORES - 1):
             wait(all_v, send_b)
+
+    if detour:
+
+        @pl.when(relays)
+        def _():
+            wait(relay_v, send_r)
 
     @pl.when(core < CORES - 1)
     def _():
@@ -552,13 +592,14 @@
             pltpu.VMEM((rank, maps), up_key.dtype),
             pltpu.VMEM((rank, maps), up_value.dtype),
             pltpu.VMEM((n, block_len, width), latent.dtype),
+            pltpu.VMEM((CORES, block_len, width), latent.dtype),
             pltpu.VMEM((part_rows, head_dim), jnp.float32),
             pltpu.VMEM((seqs // CORES, grps, CORES, part_rows, head_dim), jnp.float32),
             dma((6,)),
         ]
         + [dma] * 4
         + [dma((grps,))]
-        + [dma] * 8
+        + [dma] * 10
         + [pltpu.SemaphoreType.REGULAR] * 6,
         compiler_params=pltpu.CompilerParams(collective_id=0, has_side_effects=True),
         name="exchange",

time: 18 us -> 17.8 us (0.989)
  the two profiles are of different devices: /device:TPU:13 before, /device:TPU:8 now
where the time goes in v6:
time: 17.8 us; the launch traced here: 17.6 us
  Pallas kernels  16.9 us (95%)
  between operations  0.64 us (4%)
    pallas_call x1, Pallas kernels, body(): pl.pallas_call(functools.partial(kernel, grps, seqs, per_seq, per_group,...  16.1 us
    pallas_call x1, Pallas kernels, body(): pl.pallas_call(write_kernel, out_shape=(jax.ShapeDtypeStruct(received.sha...  0.89 us

profile of v6, /device:TPU:8, one launch (start us, length us, event | category | flops | bytes accessed | tf_op | source)
XLA Modules:
  0.0 17.6 jit_solution(12816153971150876053)
XLA Ops:
  0.6 16.1 %exchange.1 = (bf16[32,32,256]{2,1,0:T(8,128)(2,1)S(1)}, f32[8,8192]{1,0:T(8,128)S(1)}) custom-call(s32[256]{0:T(256)} %dest_hbm.1, s32[8]{0:T(128)} %len_hbm.1, bf16[1,32,32,256]{3,2,1,0:T(8,128)(2,1)} %lat_hbm.1, bf16[8,64,128]{2,1,0:T(8,128)(2,1)} %q_hbm.1, bf16[4,128,256]{2,1,0:T(8,128)(2,1)} %uk_hbm.1, bf16[4,128,256]{2,1,0:T(8,128)(2,1)} %uv_hbm.1), custom_call_target="tpu_custom_call" | custom-call | tf_op jit(solution)/shard_map/exchange/pallas_call | solution.py:578
  16.7 0.9 %write_out.1 = (bf16[32,32,256]{2,1,0:T(8,128)(2,1)}, f32[8,8192]{1,0:T(8,128)}) custom-call(bf16[32,32,256]{2,1,0:T(8,128)(2,1)S(1)} %get-tuple-element.6.recv_ref, f32[8,8192]{1,0:T(8,128)S(1)} %get-tuple-element.7.att_ref), custom_call_target="tpu_custom_call" | custom-call | tf_op jit(solution)/shard_map/write_out/pallas_call | solution.py:607

commit v7 on v6

--- a/solution.py
+++ b/solution.py
@@ -98,20 +98,10 @@
     part_v,
     all_v,
     in_sems,
-    send_a,
-    recv_near,
-    recv_far,
-    send_z,
+    recv_a,
     recv_z,
-    send_p,
     recv_p,
-    send_c,
     recv_c,
-    send_b,
-    recv_b,
-    send_x,
-    send_d,
-    send_r,
     recv_r,
     plane_sem,
     line_sem,
@@ -138,6 +128,7 @@
     slots, block_len, width = lat_v.shape
     heads, head_dim = q_v.shape
     barrier = pltpu.get_barrier_semaphore()
+    sends = in_sems.at[0]
 
     def signal(sem, there):
         pl.semaphore_signal(sem, inc=1, device_id=there, device_id_type=MESH)
@@ -168,7 +159,7 @@
         (uv_hbm.at[group], uv_v),
         (len_hbm, len_s),
     ]
-    loads = [pltpu.make_async_copy(src, dst, in_sems.at[i]) for i, (src, dst) in enumerate(loads)]
+    loads = [pltpu.make_async_copy(src, dst, in_sems.at[min(i, 2)]) for i, (src, dst) in enumerate(loads)]
     for load in loads[:2]:
         load.start()
 
@@ -248,7 +239,7 @@
         recv_ref[me] = out_v[me]
 
     def block(to_group, to_shard, recv_sem):
-        send(out_v.at[to_group * seqs + to_shard], recv_ref.at[me], (to_group, to_shard), send_a, recv_sem)
+        send(out_v.at[to_group * seqs + to_shard], recv_ref.at[me], (to_group, to_shard), sends, recv_sem)
 
     def turn(table, k):
         if table is None:
@@ -271,7 +262,7 @@
         for k in range(first, end):
             to_spot = turn(turns, k)
             for c in range(CORES):
-                block(first_far + j, to_spot * CORES + lax.rem(core + c, CORES), recv_far)
+                block(first_far + j, to_spot * CORES + lax.rem(core + c, CORES), recv_a)
 
     detour = lower_turns is not None and half > 1
     turns_off = (group == half - 1 + side) & (spot == chips - 1) & (core == side)
@@ -296,14 +287,14 @@
                 source_row = group * seqs + (chips - 1) * CORES + core
                 for c in range(CORES):
                     there = (off_group, off_spot * CORES + c)
-                    send(relay_v.at[c], recv_ref.at[source_row], there, send_r, recv_far)
+                    send(relay_v.at[c], recv_ref.at[source_row], there, sends, recv_a)
 
     def near_blocks(lowest, highest):
         @pl.loop(lowest, highest)
         def _(g):
             @pl.loop(0, seqs)
             def _(k):
-                block(g, lax.rem(shard + k, seqs), recv_near)
+                block(g, lax.rem(shard + k, seqs), recv_a)
 
     @pl.when(side == 1)
     def _():
@@ -329,11 +320,11 @@
 
     @pl.loop(side * half, group)
     def _(g):
-        send(part_v, all_v.at[spot, group, core], (g, spot * CORES + CORES - 1), send_d, recv_z.at[group])
+        send(part_v, all_v.at[spot, group, core], (g, spot * CORES + CORES - 1), sends, recv_z.at[group])
 
     @pl.when(core < CORES - 1)
     def _():
-        send(part_v, all_v.at[spot, group, core], (group, spot * CORES + CORES - 1), send_c, recv_c)
+        send(part_v, all_v.at[spot, group, core], (group, spot * CORES + CORES - 1), sends, recv_c)
 
     @pl.when(leads)
     def _():
@@ -357,20 +348,20 @@
         def _():
             for c in range(CORES):
                 held = out_v.at[off_group * seqs + off_spot * CORES + c]
-                send(held, relay_v.at[c], (group, core), send_a, recv_r)
+                send(held, relay_v.at[c], (group, core), sends, recv_r)
 
     @pl.loop(1, seqs)
     def _(k):
-        block(group, lax.rem(shard + k, seqs), recv_near)
+        block(group, lax.rem(shard + k, seqs), recv_a)
 
     def along_line(g):
         both = all_v.at[spot, group]
-        send(both, both, (g, shard), send_z, recv_z.at[group])
+        send(both, both, (g, shard), sends, recv_z.at[group])
 
     def over_plane(g):
         both = all_v.at[spot, g]
         for k in range(1, chips):
-            send(both, both, (group, lax.rem(spot + k, chips) * CORES + core), send_p, recv_p)
+            send(both, both, (group, lax.rem(spot + k, chips) * CORES + core), sends, recv_p)
 
     def release():
         @pl.when(leads)
@@ -425,7 +416,7 @@
                 crossed = all_v.at[spot, g]
                 for i in range(1, half):
                     to_group = side * half + lax.rem(group - side * half + i, half)
-                    send(crossed, crossed, (to_group, shard), send_x, recv_z.at[g])
+                    send(crossed, crossed, (to_group, shard), sends, recv_z.at[g])
                 over_plane(g)
 
     @pl.when(side == 1)
@@ -487,12 +478,12 @@
         with jax.named_scope("w_p"):
             wait(all_v.at[pl.ds(0, chips - 1)], recv_p)
         for c in range(CORES - 1):
-            send(all_v, all_v, (group, spot * CORES + c), send_b, recv_b)
+            send(all_v, all_v, (group, spot * CORES + c), sends, recv_c)
 
     @pl.when(core < CORES - 1)
     def _():
         with jax.named_scope("w_c"):
-            wait(all_v, recv_b)
+            wait(all_v, recv_c)
 
     batch = att_ref.shape[0]
     with jax.named_scope("att"):
@@ -510,48 +501,46 @@
                 att_ref[:, at : at + head_dim] = held[h]
 
     with jax.named_scope("w_send"):
-        wait(recv_ref.at[pl.ds(0, n - 1)], send_a)
+        wait(recv_ref.at[pl.ds(0, n - 1)], sends)
 
     @pl.when(leads)
     def _():
         @pl.loop(0, half - (group - side * half))
         def _(_):
-            wait(all_v.at[0, 0], send_z)
+            wait(all_v.at[0, 0], sends)
 
 
         @pl.when(outer)
         def _():
             for _ in range(half - 1):
-                wait(all_v.at[0, pl.ds(0, half)], send_x)
-
-        wait(all_v.at[pl.ds(0, chips - 1)], send_p)
+                wait(all_v.at[0, pl.ds(0, half)], sends)
+
+        wait(all_v.at[pl.ds(0, chips - 1)], sends)
         for c in range(CORES - 1):
-            wait(all_v, send_b)
+            wait(all_v, sends)
 
     if detour:
 
         @pl.when(relays)
         def _():
-            wait(relay_v, send_r)
+            wait(relay_v, sends)
 
     @pl.when(core < CORES - 1)
     def _():
-        wait(part_v, send_c)
+        wait(part_v, sends)
 
     @pl.loop(side * half, group)
     def _(_):
-        wait(part_v, send_d)
-
-    with jax.named_scope("w_near"):
-        wait(recv_ref.at[pl.ds(0, n // 2 - 1)], recv_near)
+        wait(part_v, sends)
+
     with jax.named_scope("w_far"):
-        wait(recv_ref.at[pl.ds(0, n // 2)], recv_far)
-
-
-def write_kernel(recv_ref, att_ref, latent_out, attended_out, sems):
+        wait(recv_ref.at[pl.ds(0, n - 1)], recv_a)
+
+
+def write_kernel(recv_ref, att_ref, latent_out, attended_out, sem):
     copies = [
-        pltpu.make_async_copy(recv_ref, latent_out, sems.at[0]),
-        pltpu.make_async_copy(att_ref, attended_out, sems.at[1]),
+        pltpu.make_async_copy(recv_ref, latent_out, sem),
+        pltpu.make_async_copy(att_ref, attended_out, sem),
     ]
     for copy in copies:
         copy.start()
@@ -595,11 +584,11 @@
             pltpu.VMEM((CORES, block_len, width), latent.dtype),
             pltpu.VMEM((part_rows, head_dim), jnp.float32),
             pltpu.VMEM((seqs // CORES, grps, CORES, part_rows, head_dim), jnp.float32),
-            dma((6,)),
+            dma((3,)),
+            dma,
+            dma((grps,)),
         ]
-        + [dma] * 4
-        + [dma((grps,))]
-        + [dma] * 10
+        + [dma] * 3
         + [pltpu.SemaphoreType.REGULAR] * 6,
         compiler_params=pltpu.CompilerParams(collective_id=0, has_side_effects=True),
         name="exchange",
@@ -612,7 +601,7 @@
         ),
         in_specs=[anywhere] * 2,
         out_specs=(anywhere, anywhere),
-        scratch_shapes=[dma((2,))],
+        scratch_shapes=[dma],
         name="write_out",
     )(pltpu.with_memory_space_constraint(received, pltpu.VMEM), pltpu.with_memory_space_constraint(attended, pltpu.VMEM))
     return (decode_latent.reshape(1, groups, seqs, block_len, width), attended)

time: 17.8 us -> 17.6 us (0.989)
  no operation moved by 1% of the time
where the time goes in v7:
time: 17.6 us; the launch traced here: 17.5 us
  Pallas kernels  16.8 us (95%)
  between operations  0.64 us (4%)
    pallas_call x1, Pallas kernels, body(): pl.pallas_call(functools.partial(kernel, grps, seqs, per_seq, per_group,...  15.9 us
    pallas_call x1, Pallas kernels, body(): pl.pallas_call(write_kernel, out_shape=(jax.ShapeDtypeStruct(received.sha...  0.89 us

profile of v7, /device:TPU:8, one launch (start us, length us, event | category | flops | bytes accessed | tf_op | source)
XLA Modules:
  0.0 17.5 jit_solution(1600640502679119552)
XLA Ops:
  0.6 15.9 %exchange.1 = (bf16[32,32,256]{2,1,0:T(8,128)(2,1)S(1)}, f32[8,8192]{1,0:T(8,128)S(1)}) custom-call(s32[256]{0:T(256)} %dest_hbm.1, s32[8]{0:T(128)} %len_hbm.1, bf16[1,32,32,256]{3,2,1,0:T(8,128)(2,1)} %lat_hbm.1, bf16[8,64,128]{2,1,0:T(8,128)(2,1)} %q_hbm.1, bf16[4,128,256]{2,1,0:T(8,128)(2,1)} %uk_hbm.1, bf16[4,128,256]{2,1,0:T(8,128)(2,1)} %uv_hbm.1), custom_call_target="tpu_custom_call" | custom-call | tf_op jit(solution)/shard_map/exchange/pallas_call | solution.py:567
  16.6 0.9 %write_out.1 = (bf16[32,32,256]{2,1,0:T(8,128)(2,1)}, f32[8,8192]{1,0:T(8,128)}) custom-call(bf16[32,32,256]{2,1,0:T(8,128)(2,1)S(1)} %get-tuple-element.6.recv_ref, f32[8,8192]{1,0:T(8,128)S(1)} %get-tuple-element.7.att_ref), custom_call_target="tpu_custom_call" | custom-call | tf_op jit(solution)/shard_map/write_out/pallas_call | solution.py:596

commit v8 on v7

--- a/solution.py
+++ b/solution.py
@@ -256,7 +256,7 @@
     else:
         upper_turns = lower_turns = None
     ahead_own = (spot == 0) & (core < CORES - 1)
-    ahead = (spot > 0) & (core < CORES - 1) & (chips == 4)
+    ahead = (spot > 0) & (chips == 4)
 
     def far_blocks(turns, j, first, end):
         for k in range(first, end):
@@ -281,13 +281,15 @@
             def _():
                 far_blocks(lower_turns, half - 1, chips - 1, chips)
 
+            @pl.when(turns_off)
+            def _():
+                block(off_group, off_spot * CORES + 0, recv_a)
+
             @pl.when(relays)
             def _():
                 wait(relay_v, recv_r)
                 source_row = group * seqs + (chips - 1) * CORES + core
-                for c in range(CORES):
-                    there = (off_group, off_spot * CORES + c)
-                    send(relay_v.at[c], recv_ref.at[source_row], there, sends, recv_a)
+                send(relay_v, recv_ref.at[source_row], (off_group, off_spot * CORES + 1), sends, recv_a)
 
     def near_blocks(lowest, highest):
         @pl.loop(lowest, highest)
@@ -346,9 +348,8 @@
 
         @pl.when(turns_off)
         def _():
-            for c in range(CORES):
-                held = out_v.at[off_group * seqs + off_spot * CORES + c]
-                send(held, relay_v.at[c], (group, core), sends, recv_r)
+            held = out_v.at[off_group * seqs + off_spot * CORES + 1]
+            send(held, relay_v, (group, core), sends, recv_r)
 
     @pl.loop(1, seqs)
     def _(k):
@@ -581,7 +582,7 @@
             pltpu.VMEM((rank, maps), up_key.dtype),
             pltpu.VMEM((rank, maps), up_value.dtype),
             pltpu.VMEM((n, block_len, width), latent.dtype),
-            pltpu.VMEM((CORES, block_len, width), latent.dtype),
+            pltpu.VMEM((block_len, width), latent.dtype),
             pltpu.VMEM((part_rows, head_dim), jnp.float32),
             pltpu.VMEM((seqs // CORES, grps, CORES, part_rows, head_dim), jnp.float32),
             dma((3,)),

time: 17.6 us -> 17.5 us (level)
  the two profiles are of different devices: /device:TPU:8 before, /device:TPU:13 now
where the time goes in v8:
time: 17.5 us; the launch traced here: 17.1 us
  Pallas kernels  16.5 us (94%)
  between operations  0.64 us (4%)
    pallas_call x1, Pallas kernels, body(): pl.pallas_call(functools.partial(kernel, grps, seqs, per_seq, per_group,...  15.6 us
    pallas_call x1, Pallas kernels, body(): pl.pallas_call(write_kernel, out_shape=(jax.ShapeDtypeStruct(received.sha...  0.89 us

profile of v8, /device:TPU:13, one launch (start us, length us, event | category | flops | bytes accessed | tf_op | source)
XLA Modules:
  0.0 17.1 jit_solution(4739595505289516246)
XLA Ops:
  0.6 15.6 %exchange.1 = (bf16[32,32,256]{2,1,0:T(8,128)(2,1)S(1)}, f32[8,8192]{1,0:T(8,128)S(1)}) custom-call(s32[256]{0:T(256)} %dest_hbm.1, s32[8]{0:T(128)} %len_hbm.1, bf16[1,32,32,256]{3,2,1,0:T(8,128)(2,1)} %lat_hbm.1, bf16[8,64,128]{2,1,0:T(8,128)(2,1)} %q_hbm.1, bf16[4,128,256]{2,1,0:T(8,128)(2,1)} %uk_hbm.1, bf16[4,128,256]{2,1,0:T(8,128)(2,1)} %uv_hbm.1), custom_call_target="tpu_custom_call" | custom-call | tf_op jit(solution)/shard_map/exchange/pallas_call | solution.py:568
  16.3 0.9 %write_out.1 = (bf16[32,32,256]{2,1,0:T(8,128)(2,1)}, f32[8,8192]{1,0:T(8,128)}) custom-call(bf16[32,32,256]{2,1,0:T(8,128)(2,1)S(1)} %get-tuple-element.6.recv_ref, f32[8,8192]{1,0:T(8,128)S(1)} %get-tuple-element.7.att_ref), custom_call_target="tpu_custom_call" | custom-call | tf_op jit(solution)/shard_map/write_out/pallas_call | solution.py:597

commit v9 on v8

--- a/solution.py
+++ b/solution.py
@@ -102,11 +102,9 @@
     recv_z,
     recv_p,
     recv_c,
-    recv_r,
     plane_sem,
     line_sem,
     all_sem,
-    go_sem,
     top_sem,
     mid_sem,
 ):
@@ -287,7 +285,7 @@
 
             @pl.when(relays)
             def _():
-                wait(relay_v, recv_r)
+                wait(relay_v, recv_z.at[group])
                 source_row = group * seqs + (chips - 1) * CORES + core
                 send(relay_v, recv_ref.at[source_row], (off_group, off_spot * CORES + 1), sends, recv_a)
 
@@ -349,7 +347,7 @@
         @pl.when(turns_off)
         def _():
             held = out_v.at[off_group * seqs + off_spot * CORES + 1]
-            send(held, relay_v, (group, core), sends, recv_r)
+            send(held, relay_v, (group, core), sends, recv_z.at[group])
 
     @pl.loop(1, seqs)
     def _(k):
@@ -367,13 +365,7 @@
     def release():
         @pl.when(leads)
         def _():
-            for c in range(CORES - 1):
-                signal(go_sem, (group, spot * CORES + c))
             over_plane(group)
-
-        @pl.when(core < CORES - 1)
-        def _():
-            pl.semaphore_wait(go_sem, 1)
 
     @pl.when(core < CORES - 1)
     def _():
@@ -589,8 +581,8 @@
             dma,
             dma((grps,)),
         ]
-        + [dma] * 3
-        + [pltpu.SemaphoreType.REGULAR] * 6,
+        + [dma] * 2
+        + [pltpu.SemaphoreType.REGULAR] * 5,
         compiler_params=pltpu.CompilerParams(collective_id=0, has_side_effects=True),
         name="exchange",
     )(block_dest, lengths, latent, queries, up_key, up_value)

time: 17.5 us -> 17.4 us (level)
  no operation moved by 1% of the time
where the time goes in v9:
time: 17.4 us; the launch traced here: 17.1 us
  Pallas kernels  16.5 us (95%)
  between operations  0.64 us (4%)
    pallas_call x1, Pallas kernels, body(): pl.pallas_call(functools.partial(kernel, grps, seqs, per_seq, per_group,...  15.6 us
    pallas_call x1, Pallas kernels, body(): pl.pallas_call(write_kernel, out_shape=(jax.ShapeDtypeStruct(received.sha...  0.89 us

profile of v9, /device:TPU:13, one launch (start us, length us, event | category | flops | bytes accessed | tf_op | source)
XLA Modules:
  0.0 17.1 jit_solution(886858261281570704)
XLA Ops:
  0.6 15.6 %exchange.1 = (bf16[32,32,256]{2,1,0:T(8,128)(2,1)S(1)}, f32[8,8192]{1,0:T(8,128)S(1)}) custom-call(s32[256]{0:T(256)} %dest_hbm.1, s32[8]{0:T(128)} %len_hbm.1, bf16[1,32,32,256]{3,2,1,0:T(8,128)(2,1)} %lat_hbm.1, bf16[8,64,128]{2,1,0:T(8,128)(2,1)} %q_hbm.1, bf16[4,128,256]{2,1,0:T(8,128)(2,1)} %uk_hbm.1, bf16[4,128,256]{2,1,0:T(8,128)(2,1)} %uv_hbm.1), custom_call_target="tpu_custom_call" | custom-call | tf_op jit(solution)/shard_map/exchange/pallas_call | solution.py:560
  16.2 0.9 %write_out.1 = (bf16[32,32,256]{2,1,0:T(8,128)(2,1)}, f32[8,8192]{1,0:T(8,128)}) custom-call(bf16[32,32,256]{2,1,0:T(8,128)(2,1)S(1)} %get-tuple-element.6.recv_ref, f32[8,8192]{1,0:T(8,128)S(1)} %get-tuple-element.7.att_ref), custom_call_target="tpu_custom_call" | custom-call | tf_op jit(solution)/shard_map/write_out/pallas_call | solution.py:589
